TPU v7x, 256 devices: a whole 4x4x8 slice. The times are simulated.
256 devices in a mesh: nodes: 32 (over y, z_lo, x), orb: 8 (over z_hi, core).
Axes of the slice: x: 4, y: 4, z: 8 (z_hi: 4, z_lo: 2; z = z_hi * 2 + z_lo), core: 2. Of those that a mesh axis runs over, the one named last changes fastest.
Arguments:
- orbitals: float32 [20736, 2048], P('nodes', 'orb'), may hold values from -60 to 60
- cell_matrix: float32 [32, 729, 729], P('nodes'), may hold values from -0.25 to 1.75
- connectivity: int32 [32, 729], P('nodes'), may hold values from 0 to 728, as said below
- face_nodes: int32 [2592], P('nodes'), may hold values from 0 to 647, as said below
Outputs:
- rotated: float32 [20736, 2048], P('nodes', 'orb')
Inputs may be any that keep to these rules, and one draw needn't show every extreme that they name: `connectivity`: within a section, entries below 648 are local node numbers and entry 648 + g is ghost slot g; the entries of one cell are distinct, and every local node and every ghost slot of a section appears in some cell of it. Ghost slots appear only in the last cell of a section. `face_nodes`: the 81 entries of a section are distinct local node numbers, listed in the order of the ghost slots of the section below.
All inputs are finite; a program needn't handle non-finite values.
Results may differ from a plain program's by a relative error of at most 0.000088.
Values sent between devices are 32-bit elements; how exact they have to be, the bound alone decides.
A program may use at most 64 MiB of HBM per device.

v0:
```python
import functools

import jax
import jax.numpy as jnp
from jax import lax
from jax.experimental import pallas as pl
from jax.experimental.pallas import tpu as pltpu
from jax.sharding import PartitionSpec as P

DEGREE = 8
lowest = -1.0
cutoff = 1.5
ceiling = 4.5
eps_norm = 1e-06

F32 = jnp.float32
BF16 = jnp.bfloat16
MESH = pl.DeviceIdType.MESH

OWN = 648
CELL = 729
FACE = 81
TOTAL_ROWS = 20736
W = 256
HALF = 128
KP = 768
LOW = 567
REG_L = 560
REG_G = 648
REG = 88
REG_END = 736
INT = 560
CUT = 512
ROWS = 656
PART = 320


def coefficients():
    half_width = (ceiling - cutoff) / 2.0
    centre = (ceiling + cutoff) / 2.0
    sigma_one = half_width / (lowest - centre)
    table = [(sigma_one / half_width, 0.0)]
    now = sigma_one
    for _ in range(DEGREE - 1):
        nxt = 1.0 / (2.0 / sigma_one - now)
        table.append((2.0 * nxt / half_width, now * nxt))
        now = nxt
    return centre, table


CENTRE, TABLE = coefficients()


def chosen(t, which):
    if isinstance(t, int):
        return TABLE[t][which]
    value = jnp.float32(TABLE[0][which])
    for step in range(1, DEGREE):
        value = jnp.where(t == step, jnp.float32(TABLE[step][which]), value)
    return value


def split2(value):
    high = value.astype(BF16)
    low = (value - high.astype(F32)).astype(BF16)
    return high, low


def dot(left, right):
    return jnp.dot(left, right, preferred_element_type=F32)


def dot_nt(left, right):
    return lax.dot_general(left, right, (((1,), (1,)), ((), ())), preferred_element_type=F32)


def iota(shape, dim):
    return lax.broadcasted_iota(jnp.int32, shape, dim)


def one_hot(position, shape, dim):
    return jnp.where(iota(shape, dim).astype(F32) == position, 1.0, 0.0).astype(BF16)


def kernel(
    x_ref, a_ref, conn_ref, faces_ref, out_ref,
    irow, q, ah, al, bh, bl, mh, ml, qt, vcat, vbuf, xs, pre, pf,
    send_l, send_g, from_above, from_below,
    fall, ta_h, ta_l, tb_h, tb_l, stage_h, stage_l, acc, rot_h, rot_l,
    tiles, arrived, mine, ex0, ex1, ex2, final, gathered, norms, nown, scales,
    halo_send, halo_recv, z_send, z_recv, d_send, d_recv,
    rs_send, rs_recv, ex_send, ex_recv, ag_send, ag_recv, n_send, n_recv, s_send, s_recv,
):
    node = lax.axis_index("nodes")
    orb = lax.axis_index("orb")
    a = orb // 2
    c = orb % 2
    zl = (node // 4) % 2
    xy = (node // 8) * 4 + node % 4
    flip = node + 4 - 8 * zl
    up = (node + 1) % 32
    down = (node + 31) % 32
    has_above = jnp.where(node < 31, jnp.float32(1.0), jnp.float32(0.0))
    has_below = jnp.where(node > 0, jnp.float32(1.0), jnp.float32(0.0))

    def orb_at(da, dc):
        other = c if dc == 0 else 1 - c
        return ((a + da) % 4) * 2 + other

    def node_of(position, z):
        return (position // 4) * 8 + z * 4 + position % 4

    barrier = pltpu.get_barrier_semaphore()

    def greet(k, _):
        pl.semaphore_signal(barrier, inc=1, device_id=((node + k) % 32, orb), device_id_type=MESH)
        return 0

    lax.fori_loop(1, 32, greet, 0)
    for k in range(1, 8):
        pl.semaphore_signal(barrier, inc=1, device_id=(node, orb_at(k // 2, k % 2)), device_id_type=MESH)
    for k in range(2, 8):
        pl.semaphore_signal(barrier, inc=1, device_id=(flip, orb_at(k // 2, k % 2)), device_id_type=MESH)

    irow[...] = jnp.full(irow.shape, 100000, jnp.int32)
    irow[0:1, 0:FACE] = faces_ref[...]
    face_row = irow[0:1, 0:128].astype(F32)
    irow[8:9, 0:CELL] = conn_ref[...]
    entry = irow[8:9, :].astype(F32)
    square = (128, 128)
    face_col = jnp.sum(
        jnp.where(iota(square, 0) == iota(square, 1), jnp.broadcast_to(face_row, square), 0.0), axis=1, keepdims=True
    )

    def position_row(number):
        shape = (128, KP)
        same = number == face_col
        hit = jnp.sum(jnp.where(same, iota(shape, 0).astype(F32) + 1.0, 0.0), axis=0, keepdims=True)
        below = jnp.sum(jnp.where(face_col < number, 1.0, 0.0), axis=0, keepdims=True)
        return jnp.where(hit > 0.0, LOW - 1.0 + hit, number - below)

    local = iota((1, KP), 1).astype(F32)
    local_pos = jnp.where(local < OWN, position_row(local), -1.0)
    cell_pos = jnp.where(entry < OWN, position_row(entry), jnp.where(entry < CELL, entry + 7.0, -1.0))

    q[...] = one_hot(local_pos, (KP, KP), 0)
    xs[...] = jnp.zeros(xs.shape, F32)
    xs[0:OWN, :] = x_ref[...]
    start = xs[...]
    x1 = start.astype(BF16)
    rest = start - x1.astype(F32)
    x2 = rest.astype(BF16)
    x3 = (rest - x2.astype(F32)).astype(BF16)
    vbuf[0, ...] = (dot(q[...], x1) + dot(q[...], x2)) + dot(q[...], x3)
    vbuf[1, ...] = jnp.zeros((KP, W), F32)

    pl.semaphore_wait(barrier, 31 + 7 + 6)

    def columns(chunk):
        return slice(chunk * HALF, (chunk + 1) * HALF)

    def halo(t, chunk, way):
        slot = (t + 2) % 2
        if way == 0:
            src, dst, target = send_l, from_above, down
        else:
            src, dst, target = send_g, from_below, up
        return pltpu.make_async_remote_copy(
            src_ref=src.at[slot, chunk],
            dst_ref=dst.at[slot, chunk],
            send_sem=halo_send.at[slot, chunk, way],
            recv_sem=halo_recv.at[slot, chunk, way],
            device_id=(target, orb),
            device_id_type=MESH,
        )

    for chunk in range(2):
        send_l[1, chunk] = vbuf[0, REG_L:REG_G, columns(chunk)]
        halo(-1, chunk, 0).start()

    q[...] = one_hot(cell_pos, (KP, KP), 0)
    xs_rows = a_ref[...]
    high, low = split2(xs_rows)
    ah[...] = jnp.zeros(ah.shape, BF16)
    al[...] = jnp.zeros(al.shape, BF16)
    ah[0:CELL, 0:CELL] = high
    al[0:CELL, 0:CELL] = low
    bh[...] = dot(q[...], ah[...]).astype(BF16)
    bl[...] = dot(q[...], al[...]).astype(BF16)
    mh[...] = dot_nt(bh[...], q[...]).astype(BF16)
    ml[...] = dot_nt(bl[...], q[...]).astype(BF16)

    reg_row = iota((REG, HALF), 0)
    mask = jnp.where(reg_row >= 7, 1.0, 0.0).astype(F32) * has_above

    def put(chunk, low_row, high_row, value):
        high, low = split2(value)
        vcat[chunk, low_row:high_row, 0:HALF] = high
        vcat[chunk, low_row:high_row, HALF:W] = low

    def product(chunk, rows, depth):
        both = dot(mh[rows, depth], vcat[chunk, depth, :])
        third = dot(ml[rows, depth], vcat[chunk, depth, 0:HALF])
        return (both[:, 0:HALF] + both[:, HALF:W]) + third

    def prepare(chunk):
        pre[chunk] = product(chunk, slice(INT, REG_END), slice(0, CUT))

    for chunk in range(2):
        put(chunk, 0, KP, vbuf[0, :, columns(chunk)])
        prepare(chunk)

    def faces_out(t, chunk):
        value = pre[chunk] + product(chunk, slice(INT, REG_END), slice(CUT, KP))
        pf[chunk] = value
        slot = (t + 2) % 2
        send_l[slot, chunk] = value[0:REG]
        send_g[slot, chunk] = value[REG : 2 * REG]
        halo(t, chunk, 0).start()
        halo(t, chunk, 1).start()

    def interior(t, chunk):
        now, old = t % 2, (t + 1) % 2
        total = product(chunk, slice(0, INT), slice(0, KP))
        cols = columns(chunk)
        fresh = (total - CENTRE * vbuf[now, 0:INT, cols]) * chosen(t, 0) - chosen(t, 1) * vbuf[old, 0:INT, cols]
        vbuf[old, 0:INT, cols] = fresh
        put(chunk, 0, INT, fresh)

    def faces_in(t, chunk):
        now, old = t % 2, (t + 1) % 2
        slot = t % 2
        halo(t, chunk, 0).wait_recv()
        halo(t, chunk, 1).wait_recv()
        cols = columns(chunk)
        lower = pf[chunk, 0:REG] + from_below[slot, chunk] * has_below
        upper = (pf[chunk, REG : 2 * REG] + from_above[slot, chunk]) * mask
        for rows, total in ((slice(REG_L, REG_G), lower), (slice(REG_G, REG_END), upper)):
            fresh = (total - CENTRE * vbuf[now, rows, cols]) * chosen(t, 0) - chosen(t, 1) * vbuf[old, rows, cols]
            vbuf[old, rows, cols] = fresh
            put(chunk, rows.start, rows.stop, fresh)

    def close(t):
        for chunk in range(2):
            halo(t, chunk, 0).wait_send()
            halo(t, chunk, 1).wait_send()

    for chunk in range(2):
        halo(-1, chunk, 0).wait_recv()
        ghost = from_above[1, chunk] * mask
        vbuf[0, REG_G:REG_END, columns(chunk)] = ghost
        put(chunk, REG_G, REG_END, ghost)
        faces_out(0, chunk)
    for chunk in range(2):
        interior(0, chunk)
        prepare(chunk)
    for chunk in range(2):
        halo(-1, chunk, 0).wait_send()
    close(0)

    def step(t, _):
        for chunk in range(2):
            faces_in(t - 1, chunk)
            faces_out(t, chunk)
        for chunk in range(2):
            interior(t, chunk)
            prepare(chunk)
        close(t)
        return 0

    lax.fori_loop(1, DEGREE, step, 0)
    for chunk in range(2):
        faces_in(DEGREE - 1, chunk)

    fall[0, 0:OWN, :] = vbuf[DEGREE % 2, 0:OWN, :]
    own = fall[0, 0:OWN, :]
    nown[0] = jnp.sum(own * own, axis=0, keepdims=True)
    norms[node] = nown[0]

    def norm_copy(k):
        return pltpu.make_async_remote_copy(
            src_ref=nown.at[0],
            dst_ref=norms.at[node],
            send_sem=n_send,
            recv_sem=n_recv,
            device_id=((node + k) % 32, orb),
            device_id_type=MESH,
        )

    def norm_start(k, _):
        norm_copy(k).start()
        return 0

    lax.fori_loop(1, 32, norm_start, 0)

    first, second = slice(0, PART), slice(PART, OWN)

    def z_copy(index):
        src, dst, rows, da = (
            (0, 6, first, 1),
            (0, 2, second, -1),
            (6, 4, first, 1),
            (2, 4, second, -1),
            (0, 6, second, 1),
            (0, 2, first, -1),
        )[index]
        return pltpu.make_async_remote_copy(
            src_ref=fall.at[src, rows],
            dst_ref=fall.at[dst, rows],
            send_sem=z_send.at[index],
            recv_sem=z_recv.at[index],
            device_id=(node, orb_at(da, 0)),
            device_id_type=MESH,
        )

    def d_copy(index):
        slot, rows = (
            (0, slice(0, OWN)),
            (6, first),
            (2, second),
            (4, first),
            (4, second),
            (6, second),
            (2, first),
        )[index]
        return pltpu.make_async_remote_copy(
            src_ref=fall.at[slot, rows],
            dst_ref=fall.at[slot + 1, rows],
            send_sem=d_send.at[index],
            recv_sem=d_recv.at[index],
            device_id=(node, orb_at(0, 1)),
            device_id_type=MESH,
        )

    z_copy(0).start()
    z_copy(1).start()
    d_copy(0).start()
    for k in range(8):
        fall[k, OWN:ROWS, :] = jnp.zeros((ROWS - OWN, W), F32)
    stage_h[...] = jnp.zeros(stage_h.shape, BF16)
    stage_l[...] = jnp.zeros(stage_l.shape, BF16)

    padded = (384, W)
    top = jnp.where(iota(padded, 0) < PART, fall[0, 0:384, :], 0.0)
    ta_h[...], ta_l[...] = split2(top.T)
    xs[...] = jnp.zeros(xs.shape, F32)
    xs[0 : OWN - PART, :] = fall[0, PART:OWN, :]
    tb_h[...], tb_l[...] = split2(xs[0:384, :].T)

    def half_gram(which, slot):
        rows = first if which == 0 else second
        high, low = split2(fall[slot, rows, :])
        count = rows.stop - rows.start
        stage_h[which, 0:count, :] = high
        stage_l[which, 0:count, :] = low
        left_h, left_l = (ta_h, ta_l) if which == 0 else (tb_h, tb_l)
        return (dot(left_h[...], stage_h[which]) + dot(left_h[...], stage_l[which])) + dot(left_l[...], stage_h[which])

    def keep(tile, value):
        tiles[tile] = value.reshape(16, 16, W)

    def rs_copy(group, k):
        lo, hi = ((0, 2), (2, 6), (6, 7))[group]
        other = xy ^ k
        return pltpu.make_async_remote_copy(
            src_ref=tiles.at[lo:hi, other],
            dst_ref=arrived.at[lo:hi, xy],
            send_sem=rs_send.at[group],
            recv_sem=rs_recv.at[group],
            device_id=(node_of(other, zl), orb),
            device_id_type=MESH,
        )

    def rs_start(group):
        def one(k, _):
            rs_copy(group, k).start()
            return 0

        lax.fori_loop(1, 16, one, 0)

    def rs_sum(group):
        lo, hi = ((0, 2), (2, 6), (6, 7))[group]
        whole = arrived.at[lo:hi, 0:15]
        pltpu.make_async_copy(whole, whole, rs_recv.at[group]).wait()
        for tile in range(lo, hi):
            arrived[tile, xy] = tiles[tile, xy]
            mine[tile] = jnp.sum(arrived[tile], axis=0)

    keep(0, half_gram(0, 0) + half_gram(1, 0))
    d_copy(0).wait_recv()
    keep(1, half_gram(0, 1) + half_gram(1, 1))
    rs_start(0)

    whole_norms = norms.at[0:31]
    pltpu.make_async_copy(whole_norms, whole_norms, n_recv).wait()
    scales[0] = lax.rsqrt(jnp.sum(norms[...], axis=0) / TOTAL_ROWS + eps_norm)

    def scale_copy(k):
        da, dc = k // 2, k % 2
        return pltpu.make_async_remote_copy(
            src_ref=scales.at[0],
            dst_ref=scales.at[((4 - da) % 4) * 2 + dc],
            send_sem=s_send.at[k],
            recv_sem=s_recv.at[k],
            device_id=(node, orb_at(da, dc)),
            device_id_type=MESH,
        )

    for k in range(1, 8):
        scale_copy(k).start()

    z_copy(0).wait_recv()
    z_copy(2).start()
    d_copy(1).start()
    z_copy(1).wait_recv()
    z_copy(3).start()
    d_copy(2).start()
    keep(2, half_gram(0, 6))
    keep(4, half_gram(1, 2).T)
    d_copy(1).wait_recv()
    keep(3, half_gram(0, 7))
    d_copy(2).wait_recv()
    keep(5, half_gram(1, 3).T)
    rs_start(1)
    rs_sum(0)

    z_copy(2).wait_recv()
    d_copy(3).start()
    z_copy(3).wait_recv()
    d_copy(4).start()
    d_copy(3).wait_recv()
    d_copy(4).wait_recv()
    late = jnp.where(a >= 2, 1, 0)
    keep(6, half_gram(0, 4 + late) + half_gram(1, 4 + late))
    rs_start(2)
    rs_sum(1)
    rs_sum(2)

    cross = jnp.where(a >= 2, 1 - c, c)
    partner = ((a + 2) % 4) * 2 + cross
    pairs = (
        (2, 4, orb_at(-1, 0)),
        (3, 5, orb_at(-1, 1)),
        (4, 2, orb_at(1, 0)),
        (5, 3, orb_at(1, 1)),
        (6, 7, partner),
    )

    def ex_copies():
        copies = [
            pltpu.make_async_remote_copy(
                src_ref=mine.at[0:7],
                dst_ref=ex0,
                send_sem=ex_send.at[0],
                recv_sem=ex_recv.at[0],
                device_id=(flip, orb),
                device_id_type=MESH,
            )
        ]
        for index, (src, dst, who) in enumerate(pairs):
            for near in range(2):
                copies.append(
                    pltpu.make_async_remote_copy(
                        src_ref=mine.at[src],
                        dst_ref=(ex1, ex2)[near].at[dst],
                        send_sem=ex_send.at[1 + 2 * index + near],
                        recv_sem=ex_recv.at[1 + 2 * (dst if dst < 7 else 6) - 4 + near],
                        device_id=(node if near == 0 else flip, who),
                        device_id_type=MESH,
                    )
                )
        return copies

    exchange = ex_copies()
    for copy in exchange:
        copy.start()
    z_copy(4).start()
    z_copy(5).start()
    for copy in exchange:
        copy.wait_recv()
    for tile in range(8):
        if tile < 2 or tile == 6:
            final[tile] = mine[tile] + ex0[tile]
        elif tile == 7:
            final[tile] = ex1[tile] + ex2[tile]
        else:
            final[tile] = (mine[tile] + ex0[tile]) + (ex1[tile] + ex2[tile])
        gathered[tile, xy] = final[tile]

    def ag_copy(k):
        return pltpu.make_async_remote_copy(
            src_ref=final,
            dst_ref=gathered.at[0:8, xy],
            send_sem=ag_send,
            recv_sem=ag_recv,
            device_id=(node_of(xy ^ k, zl), orb),
            device_id_type=MESH,
        )

    def ag_start(k, _):
        ag_copy(k).start()
        return 0

    lax.fori_loop(1, 16, ag_start, 0)

    natural = iota((ROWS, 1), 0).astype(F32)
    face_lane = jnp.broadcast_to(face_row, (ROWS, 128))
    lane = iota((ROWS, 128), 1).astype(F32)
    hit = jnp.sum(jnp.where(face_lane == natural, lane + 1.0, 0.0), axis=1, keepdims=True)
    below = jnp.sum(jnp.where(face_lane < natural, 1.0, 0.0), axis=1, keepdims=True)
    back = jnp.where(hit > 0.0, LOW - 1.0 + hit, natural - below)
    qt[...] = one_hot(back, (ROWS, KP), 1)
    rot_h[ROWS:KP, :] = jnp.zeros((KP - ROWS, W), BF16)
    rot_l[ROWS:KP, :] = jnp.zeros((KP - ROWS, W), BF16)

    for k in range(1, 8):
        scale_copy(k).wait_recv()
    z_copy(4).wait_recv()
    d_copy(5).start()
    z_copy(5).wait_recv()
    d_copy(6).start()
    whole_tiles = gathered.at[0:8, 0:15]
    pltpu.make_async_copy(whole_tiles, whole_tiles, ag_recv).wait()

    def rotated(slot, tile, transposed):
        scale = scales[slot]
        left_h, left_l = split2(fall[slot] * (scale * scale))
        right_h, right_l = split2(gathered[tile].reshape(W, W))
        times = dot_nt if transposed else dot
        return (times(left_h, right_h) + times(left_h, right_l)) + times(left_l, right_h)

    acc[...] = rotated(0, 0, False)
    acc[...] += rotated(1, 1, True)
    acc[...] += rotated(4 + late, 6, True)
    acc[...] += rotated(5 - late, 7, False)
    acc[...] += rotated(2, 4, False)
    acc[...] += rotated(6, 2, True)
    d_copy(5).wait_recv()
    acc[...] += rotated(7, 3, True)
    d_copy(6).wait_recv()
    acc[...] += rotated(3, 5, False)
    result = (1.5 * fall[0] - (0.5 / TOTAL_ROWS) * acc[...]) * scales[0]
    high, low = split2(result)
    rot_h[0:ROWS, :] = high
    rot_l[0:ROWS, :] = low
    out = dot(qt[...], rot_h[...]) + dot(qt[...], rot_l[...])
    out_ref[...] = out[0:OWN, :]

    for index in range(6):
        z_copy(index).wait_send()
    for index in range(7):
        d_copy(index).wait_send()
    for k in range(1, 8):
        scale_copy(k).wait_send()
    pltpu.make_async_copy(whole_norms, whole_norms, n_send).wait()
    for group, (lo, hi) in enumerate(((0, 2), (2, 6), (6, 7))):
        whole = arrived.at[lo:hi, 0:15]
        pltpu.make_async_copy(whole, whole, rs_send.at[group]).wait()
    for copy in exchange:
        copy.wait_send()
    pltpu.make_async_copy(whole_tiles, whole_tiles, ag_send).wait()


def body(orbitals, cell_matrix, connectivity, face_nodes):
    vmem = pl.BlockSpec(memory_space=pltpu.VMEM)
    dma = pltpu.SemaphoreType.DMA
    return pl.pallas_call(
        kernel,
        out_shape=jax.ShapeDtypeStruct((OWN, W), F32),
        in_specs=[vmem] * 4,
        out_specs=vmem,
        scratch_shapes=[
            pltpu.VMEM((16, KP), jnp.int32),
            pltpu.VMEM((KP, KP), BF16),
            pltpu.VMEM((KP, KP), BF16),
            pltpu.VMEM((KP, KP), BF16),
            pltpu.VMEM((KP, KP), BF16),
            pltpu.VMEM((KP, KP), BF16),
            pltpu.VMEM((KP, KP), BF16),
            pltpu.VMEM((KP, KP), BF16),
            pltpu.VMEM((ROWS, KP), BF16),
            pltpu.VMEM((2, KP, W), BF16),
            pltpu.VMEM((2, KP, W), F32),
            pltpu.VMEM((KP, W), F32),
            pltpu.VMEM((2, 2 * REG, HALF), F32),
            pltpu.VMEM((2, 2 * REG, HALF), F32),
            pltpu.VMEM((2, 2, REG, HALF), F32),
            pltpu.VMEM((2, 2, REG, HALF), F32),
            pltpu.VMEM((2, 2, REG, HALF), F32),
            pltpu.VMEM((2, 2, REG, HALF), F32),
            pltpu.VMEM((8, ROWS, W), F32),
            pltpu.VMEM((W, 384), BF16),
            pltpu.VMEM((W, 384), BF16),
            pltpu.VMEM((W, 384), BF16),
            pltpu.VMEM((W, 384), BF16),
            pltpu.VMEM((2, 384, W), BF16),
            pltpu.VMEM((2, 384, W), BF16),
            pltpu.VMEM((ROWS, W), F32),
            pltpu.VMEM((KP, W), BF16),
            pltpu.VMEM((KP, W), BF16),
            pltpu.VMEM((7, 16, 16, W), F32),
            pltpu.VMEM((7, 16, 16, W), F32),
            pltpu.VMEM((7, 16, W), F32),
            pltpu.VMEM((7, 16, W), F32),
            pltpu.VMEM((8, 16, W), F32),
            pltpu.VMEM((8, 16, W), F32),
            pltpu.VMEM((8, 16, W), F32),
            pltpu.VMEM((8, 16, 16, W), F32),
            pltpu.VMEM((32, 1, W), F32),
            pltpu.VMEM((1, 1, W), F32),
            pltpu.VMEM((8, 1, W), F32),
            dma((2, 2, 2)),
            dma((2, 2, 2)),
            dma((6,)),
            dma((6,)),
            dma((7,)),
            dma((7,)),
            dma((3,)),
            dma((3,)),
            dma((11,)),
            dma((11,)),
            dma,
            dma,
            dma,
            dma,
            dma((8,)),
            dma((8,)),
        ],
        compiler_params=pltpu.CompilerParams(
            collective_id=0, has_side_effects=True, vmem_limit_bytes=60 * 1024 * 1024
        ),
    )(orbitals, cell_matrix[0], connectivity, face_nodes.reshape(1, FACE))


def solution(mesh):
    return jax.shard_map(
        body,
        mesh=mesh,
        in_specs=(P("nodes", "orb"), P("nodes", None, None), P("nodes", None), P("nodes")),
        out_specs=P("nodes", "orb"),
        check_vma=False,
    )
```

profile of v0, /device:TPU:1, one launch (start us, length us, event | category | flops | bytes accessed | tf_op | source)
XLA Modules:
  0.0 161.4 jit_solution(4046936710591041053)
XLA Ops:
  0.0 3.2 %copy.7 = f32[1,729,729]{2,1,0:T(8,128)} copy(f32[1,729,729]{2,0,1:T(1,128)} %param.5) | data formatting | bytes 4251528
  3.2 156.3 %shard_map.46 = f32[648,256]{1,0:T(8,128)} custom-call(f32[648,256]{1,0:T(8,128)} %x_ref.1, f32[729,729]{1,0:T(8,128)} %bitcast.4, s32[1,729]{1,0:T(1,128)} %conn_ref.1, s32[1,81]{1,0:T(1,128)} %bitcast.5), custom_call_target="tpu_custom_call" | custom-call | tf_op jit(solution)/shard_map/pallas_call | solution.py:567
  159.4 2.0 %copy.9 = f32[648,256]{1,0:T(8,128)} copy(f32[648,256]{1,0:T(8,128)} %shard_map.46) | data formatting | bytes 1327104
where the time goes:
time: 162 us; the launch traced here: 161 us
  Pallas kernels  156 us (96%)
  local copies, waits for them, and re-layouts  5.14 us (3%)
    pallas_call x1, Pallas kernels, body(): pl.pallas_call(kernel, out_shape=jax.ShapeDtypeStruct((OWN, W), F32), in_...  156 us
    unnamed x2, local copies, waits for them, and re-layouts  5.14 us

commit v1 on v0

--- a/solution.py
+++ b/solution.py
@@ -87,16 +87,17 @@
     irow, q, ah, al, bh, bl, mh, ml, qt, vcat, vbuf, xs, pre, pf,
     send_l, send_g, from_above, from_below,
     fall, ta_h, ta_l, tb_h, tb_l, stage_h, stage_l, acc, rot_h, rot_l,
-    tiles, arrived, mine, ex0, ex1, ex2, final, gathered, norms, nown, scales,
+    flat, flat_in, cube, cube_in, mine, ex0, ex1, ex2, final, gathered, gathered_flat, norms, nown, scales,
     halo_send, halo_recv, z_send, z_recv, d_send, d_recv,
-    rs_send, rs_recv, ex_send, ex_recv, ag_send, ag_recv, n_send, n_recv, s_send, s_recv,
+    rs_send, rs_recv, c_send, c_recv, g_send, g_recv, ex_send, ex_recv, ag_send, ag_recv, n_send, n_recv, s_send, s_recv,
 ):
     node = lax.axis_index("nodes")
     orb = lax.axis_index("orb")
     a = orb // 2
     c = orb % 2
     zl = (node // 4) % 2
-    xy = (node // 8) * 4 + node % 4
+    x, y = node % 4, node // 8
+    bits = ((x // 2 + x % 2) % 2, x // 2, (y // 2 + y % 2) % 2, y // 2)
     flip = node + 4 - 8 * zl
     up = (node + 1) % 32
     down = (node + 31) % 32
@@ -107,8 +108,15 @@
         other = c if dc == 0 else 1 - c
         return ((a + da) % 4) * 2 + other
 
-    def node_of(position, z):
-        return (position // 4) * 8 + z * 4 + position % 4
+    def number(corner):
+        return corner[3] * 8 + corner[2] * 4 + corner[1] * 2 + corner[0]
+
+    def node_of(corner):
+        there_x = corner[1] * 2 + (corner[0] + corner[1]) % 2
+        there_y = corner[3] * 2 + (corner[2] + corner[3]) % 2
+        return there_y * 8 + zl * 4 + there_x
+
+    sid = number(bits)
 
     barrier = pltpu.get_barrier_semaphore()
 
@@ -294,15 +302,19 @@
     lax.fori_loop(1, 32, norm_start, 0)
 
     first, second = slice(0, PART), slice(PART, OWN)
+    first_a, first_b = slice(0, 160), slice(160, PART)
+    second_a, second_b = slice(PART, 488), slice(488, OWN)
 
     def z_copy(index):
         src, dst, rows, da = (
             (0, 6, first, 1),
-            (0, 2, second, -1),
+            (0, 2, second, 3),
             (6, 4, first, 1),
-            (2, 4, second, -1),
-            (0, 6, second, 1),
-            (0, 2, first, -1),
+            (2, 4, second, 3),
+            (0, 6, second_a, 1),
+            (0, 2, first_a, 3),
+            (0, 6, second_b, 1),
+            (0, 2, first_b, 3),
         )[index]
         return pltpu.make_async_remote_copy(
             src_ref=fall.at[src, rows],
@@ -356,18 +368,23 @@
         left_h, left_l = (ta_h, ta_l) if which == 0 else (tb_h, tb_l)
         return (dot(left_h[...], stage_h[which]) + dot(left_h[...], stage_l[which])) + dot(left_l[...], stage_h[which])
 
+    FLAT = {0: 0, 1: 1, 6: 2}
+
     def keep(tile, value):
-        tiles[tile] = value.reshape(16, 16, W)
+        if tile in FLAT:
+            flat[FLAT[tile]] = value.reshape(16, 16, W)
+        else:
+            cube[tile - 2] = value.reshape(2, 2, 2, 2, 16, W)
 
     def rs_copy(group, k):
-        lo, hi = ((0, 2), (2, 6), (6, 7))[group]
-        other = xy ^ k
-        return pltpu.make_async_remote_copy(
-            src_ref=tiles.at[lo:hi, other],
-            dst_ref=arrived.at[lo:hi, xy],
+        lo, hi = ((0, 2), (2, 3))[group]
+        to = [(bits[d] + k // 2**d) % 2 for d in range(4)]
+        return pltpu.make_async_remote_copy(
+            src_ref=flat.at[lo:hi, number(to)],
+            dst_ref=flat_in.at[lo:hi, sid],
             send_sem=rs_send.at[group],
             recv_sem=rs_recv.at[group],
-            device_id=(node_of(other, zl), orb),
+            device_id=(node_of(to), orb),
             device_id_type=MESH,
         )
 
@@ -378,13 +395,143 @@
 
         lax.fori_loop(1, 16, one, 0)
 
+    def rs_bytes(group):
+        lo, hi = ((0, 2), (2, 3))[group]
+        return flat_in.at[lo:hi, 0:15]
+
     def rs_sum(group):
+        whole = rs_bytes(group)
+        pltpu.make_async_copy(whole, whole, rs_recv.at[group]).wait()
+        for tile, index in FLAT.items():
+            if (index == 2) == (group == 1):
+                flat_in[index, sid] = flat[index, sid]
+                mine[tile] = jnp.sum(flat_in[index], axis=0)
+
+    def cube_index(values):
+        return tuple(slice(None) if values[d] is None else values[d] for d in (3, 2, 1, 0))
+
+    def neighbour(d):
+        to = list(bits)
+        to[d] = 1 - bits[d]
+        return (node_of(to), orb)
+
+    def halving(h, j):
+        order = [(h + i) % 4 for i in range(4)]
+        src, dst = [None] * 4, [None] * 4
+        for i in range(j):
+            src[order[i]], dst[order[i]] = bits[order[i]], 1 - bits[order[i]]
+        src[order[j]] = dst[order[j]] = 1 - bits[order[j]]
+        return pltpu.make_async_remote_copy(
+            src_ref=cube.at[(h,) + cube_index(src)],
+            dst_ref=cube_in.at[(h,) + cube_index(dst)],
+            send_sem=c_send.at[h, j],
+            recv_sem=c_recv.at[h, j],
+            device_id=neighbour(order[j]),
+            device_id_type=MESH,
+        )
+
+    def halving_in(h, j):
+        order = [(h + i) % 4 for i in range(4)]
+        halving(h, j).wait_recv()
+        kept, came = [None] * 4, [None] * 4
+        for i in range(j):
+            kept[order[i]], came[order[i]] = bits[order[i]], 1 - bits[order[i]]
+        kept[order[j]] = came[order[j]] = bits[order[j]]
+        kept, came = (h,) + cube_index(kept), (h,) + cube_index(came)
+        if j < 3:
+            cube[kept] = cube[kept] + cube_in[came]
+        else:
+            mine[h + 2] = cube[kept] + cube_in[came]
+
+    def doubling(tile, j):
+        order = [(tile + i) % 4 for i in range(4)]
+        which = [None] * 4
+        for i in range(j, 4):
+            which[order[i]] = bits[order[i]]
+        where = (tile,) + cube_index(which)
+        return pltpu.make_async_remote_copy(
+            src_ref=gathered.at[where],
+            dst_ref=gathered.at[where],
+            send_sem=g_send.at[tile, j],
+            recv_sem=g_recv.at[tile, j],
+            device_id=neighbour(order[j]),
+            device_id_type=MESH,
+        )
+
+    def doubling_start(tiles, j):
+        for tile in tiles:
+            if j == 0:
+                gathered[(tile,) + cube_index(bits)] = final[tile]
+            doubling(tile, j).start()
+
+    def doubling_wait(tiles, j):
+        for tile in tiles:
+            doubling(tile, j).wait_recv()
+
+    cross = jnp.where(a >= 2, 1 - c, c)
+    partner = ((a + 2) % 4) * 2 + cross
+    late = jnp.where(a >= 2, 1, 0)
+
+    def ex_copies(group):
         lo, hi = ((0, 2), (2, 6), (6, 7))[group]
-        whole = arrived.at[lo:hi, 0:15]
-        pltpu.make_async_copy(whole, whole, rs_recv.at[group]).wait()
-        for tile in range(lo, hi):
-            arrived[tile, xy] = tiles[tile, xy]
-            mine[tile] = jnp.sum(arrived[tile], axis=0)
+        copies = [
+            pltpu.make_async_remote_copy(
+                src_ref=mine.at[lo:hi],
+                dst_ref=ex0.at[lo:hi],
+                send_sem=ex_send.at[group],
+                recv_sem=ex_recv.at[group],
+                device_id=(flip, orb),
+                device_id_type=MESH,
+            )
+        ]
+        pairs = (
+            (),
+            ((2, 4, orb_at(3, 0)), (3, 5, orb_at(3, 1)), (4, 2, orb_at(1, 0)), (5, 3, orb_at(1, 1))),
+            ((6, 7, partner),),
+        )[group]
+        for src, dst, who in pairs:
+            for near in range(2):
+                copies.append(
+                    pltpu.make_async_remote_copy(
+                        src_ref=mine.at[src],
+                        dst_ref=(ex1, ex2)[near].at[dst],
+                        send_sem=ex_send.at[2 * dst + near],
+                        recv_sem=ex_recv.at[2 * dst + near],
+                        device_id=(node if near == 0 else flip, who),
+                        device_id_type=MESH,
+                    )
+                )
+        return copies
+
+    def ex_start(group):
+        for copy in ex_copies(group):
+            copy.start()
+
+    def ex_in(group):
+        for copy in ex_copies(group):
+            copy.wait_recv()
+        for tile in ((0, 1), (2, 3, 4, 5), (6, 7))[group]:
+            if tile < 2 or tile == 6:
+                final[tile] = mine[tile] + ex0[tile]
+            elif tile == 7:
+                final[tile] = ex1[tile] + ex2[tile]
+            else:
+                final[tile] = (mine[tile] + ex0[tile]) + (ex1[tile] + ex2[tile])
+
+    def ag_copy(k):
+        to = [(bits[d] + k // 2**d) % 2 for d in range(4)]
+        return pltpu.make_async_remote_copy(
+            src_ref=final.at[6:8],
+            dst_ref=gathered_flat.at[0:2, sid],
+            send_sem=ag_send,
+            recv_sem=ag_recv,
+            device_id=(node_of(to), orb),
+            device_id_type=MESH,
+        )
+
+    def ag_start(k, _):
+        ag_copy(k).start()
+        return 0
 
     keep(0, half_gram(0, 0) + half_gram(1, 0))
     d_copy(0).wait_recv()
@@ -408,100 +555,6 @@
 
     for k in range(1, 8):
         scale_copy(k).start()
-
-    z_copy(0).wait_recv()
-    z_copy(2).start()
-    d_copy(1).start()
-    z_copy(1).wait_recv()
-    z_copy(3).start()
-    d_copy(2).start()
-    keep(2, half_gram(0, 6))
-    keep(4, half_gram(1, 2).T)
-    d_copy(1).wait_recv()
-    keep(3, half_gram(0, 7))
-    d_copy(2).wait_recv()
-    keep(5, half_gram(1, 3).T)
-    rs_start(1)
-    rs_sum(0)
-
-    z_copy(2).wait_recv()
-    d_copy(3).start()
-    z_copy(3).wait_recv()
-    d_copy(4).start()
-    d_copy(3).wait_recv()
-    d_copy(4).wait_recv()
-    late = jnp.where(a >= 2, 1, 0)
-    keep(6, half_gram(0, 4 + late) + half_gram(1, 4 + late))
-    rs_start(2)
-    rs_sum(1)
-    rs_sum(2)
-
-    cross = jnp.where(a >= 2, 1 - c, c)
-    partner = ((a + 2) % 4) * 2 + cross
-    pairs = (
-        (2, 4, orb_at(-1, 0)),
-        (3, 5, orb_at(-1, 1)),
-        (4, 2, orb_at(1, 0)),
-        (5, 3, orb_at(1, 1)),
-        (6, 7, partner),
-    )
-
-    def ex_copies():
-        copies = [
-            pltpu.make_async_remote_copy(
-                src_ref=mine.at[0:7],
-                dst_ref=ex0,
-                send_sem=ex_send.at[0],
-                recv_sem=ex_recv.at[0],
-                device_id=(flip, orb),
-                device_id_type=MESH,
-            )
-        ]
-        for index, (src, dst, who) in enumerate(pairs):
-            for near in range(2):
-                copies.append(
-                    pltpu.make_async_remote_copy(
-                        src_ref=mine.at[src],
-                        dst_ref=(ex1, ex2)[near].at[dst],
-                        send_sem=ex_send.at[1 + 2 * index + near],
-                        recv_sem=ex_recv.at[1 + 2 * (dst if dst < 7 else 6) - 4 + near],
-                        device_id=(node if near == 0 else flip, who),
-                        device_id_type=MESH,
-                    )
-                )
-        return copies
-
-    exchange = ex_copies()
-    for copy in exchange:
-        copy.start()
-    z_copy(4).start()
-    z_copy(5).start()
-    for copy in exchange:
-        copy.wait_recv()
-    for tile in range(8):
-        if tile < 2 or tile == 6:
-            final[tile] = mine[tile] + ex0[tile]
-        elif tile == 7:
-            final[tile] = ex1[tile] + ex2[tile]
-        else:
-            final[tile] = (mine[tile] + ex0[tile]) + (ex1[tile] + ex2[tile])
-        gathered[tile, xy] = final[tile]
-
-    def ag_copy(k):
-        return pltpu.make_async_remote_copy(
-            src_ref=final,
-            dst_ref=gathered.at[0:8, xy],
-            send_sem=ag_send,
-            recv_sem=ag_recv,
-            device_id=(node_of(xy ^ k, zl), orb),
-            device_id_type=MESH,
-        )
-
-    def ag_start(k, _):
-        ag_copy(k).start()
-        return 0
-
-    lax.fori_loop(1, 16, ag_start, 0)
 
     natural = iota((ROWS, 1), 0).astype(F32)
     face_lane = jnp.broadcast_to(face_row, (ROWS, 128))
@@ -513,32 +566,97 @@
     rot_h[ROWS:KP, :] = jnp.zeros((KP - ROWS, W), BF16)
     rot_l[ROWS:KP, :] = jnp.zeros((KP - ROWS, W), BF16)
 
-    for k in range(1, 8):
-        scale_copy(k).wait_recv()
-    z_copy(4).wait_recv()
-    d_copy(5).start()
-    z_copy(5).wait_recv()
-    d_copy(6).start()
-    whole_tiles = gathered.at[0:8, 0:15]
-    pltpu.make_async_copy(whole_tiles, whole_tiles, ag_recv).wait()
+    rs_sum(0)
+    ex_start(0)
+
+    z_copy(0).wait_recv()
+    z_copy(2).start()
+    d_copy(1).start()
+    z_copy(1).wait_recv()
+    z_copy(3).start()
+    d_copy(2).start()
+    keep(2, half_gram(0, 6))
+    halving(0, 0).start()
+    keep(4, half_gram(1, 2).T)
+    halving(2, 0).start()
+    d_copy(1).wait_recv()
+    keep(3, half_gram(0, 7))
+    halving(1, 0).start()
+    d_copy(2).wait_recv()
+    keep(5, half_gram(1, 3).T)
+    halving(3, 0).start()
+    early, middle = (0, 1), (2, 3, 4, 5)
+    ex_in(0)
+    doubling_start(early, 0)
+    for j in range(4):
+        for h in range(4):
+            halving_in(h, j)
+            if j < 3:
+                halving(h, j + 1).start()
+        if j == 3:
+            ex_start(1)
+            z_copy(4).start()
+            z_copy(5).start()
+        doubling_wait(early, j)
+        if j < 3:
+            doubling_start(early, j + 1)
+        if j == 2:
+            z_copy(2).wait_recv()
+            d_copy(3).start()
+            z_copy(3).wait_recv()
+            d_copy(4).start()
+
+    d_copy(3).wait_recv()
+    d_copy(4).wait_recv()
+    keep(6, half_gram(0, 4 + late) + half_gram(1, 4 + late))
+    rs_start(1)
 
     def rotated(slot, tile, transposed):
         scale = scales[slot]
         left_h, left_l = split2(fall[slot] * (scale * scale))
-        right_h, right_l = split2(gathered[tile].reshape(W, W))
+        source = gathered[tile] if tile < 6 else gathered_flat[tile - 6]
+        right_h, right_l = split2(source.reshape(W, W))
         times = dot_nt if transposed else dot
         return (times(left_h, right_h) + times(left_h, right_l)) + times(left_l, right_h)
 
+    for k in range(1, 8):
+        scale_copy(k).wait_recv()
     acc[...] = rotated(0, 0, False)
     acc[...] += rotated(1, 1, True)
-    acc[...] += rotated(4 + late, 6, True)
-    acc[...] += rotated(5 - late, 7, False)
+
+    ex_in(1)
+    doubling_start(middle, 0)
+    rs_sum(1)
+    ex_start(2)
+    z_copy(6).start()
+    z_copy(7).start()
+    doubling_wait(middle, 0)
+    doubling_start(middle, 1)
+    doubling_wait(middle, 1)
+    doubling_start(middle, 2)
+    ex_in(2)
+    gathered_flat[0, sid] = final[6]
+    gathered_flat[1, sid] = final[7]
+    lax.fori_loop(1, 16, ag_start, 0)
+    doubling_wait(middle, 2)
+    doubling_start(middle, 3)
+    z_copy(4).wait_recv()
+    z_copy(6).wait_recv()
+    d_copy(5).start()
+    z_copy(5).wait_recv()
+    z_copy(7).wait_recv()
+    d_copy(6).start()
+    doubling_wait(middle, 3)
     acc[...] += rotated(2, 4, False)
     acc[...] += rotated(6, 2, True)
     d_copy(5).wait_recv()
     acc[...] += rotated(7, 3, True)
     d_copy(6).wait_recv()
     acc[...] += rotated(3, 5, False)
+    whole_tiles = gathered_flat.at[0:2, 0:15]
+    pltpu.make_async_copy(whole_tiles, whole_tiles, ag_recv).wait()
+    acc[...] += rotated(4 + late, 6, True)
+    acc[...] += rotated(5 - late, 7, False)
     result = (1.5 * fall[0] - (0.5 / TOTAL_ROWS) * acc[...]) * scales[0]
     high, low = split2(result)
     rot_h[0:ROWS, :] = high
@@ -546,18 +664,24 @@
     out = dot(qt[...], rot_h[...]) + dot(qt[...], rot_l[...])
     out_ref[...] = out[0:OWN, :]
 
-    for index in range(6):
+    for index in range(8):
         z_copy(index).wait_send()
     for index in range(7):
         d_copy(index).wait_send()
     for k in range(1, 8):
         scale_copy(k).wait_send()
     pltpu.make_async_copy(whole_norms, whole_norms, n_send).wait()
-    for group, (lo, hi) in enumerate(((0, 2), (2, 6), (6, 7))):
-        whole = arrived.at[lo:hi, 0:15]
+    for group in range(2):
+        whole = rs_bytes(group)
         pltpu.make_async_copy(whole, whole, rs_send.at[group]).wait()
-    for copy in exchange:
-        copy.wait_send()
+    for group in range(3):
+        for copy in ex_copies(group):
+            copy.wait_send()
+    for j in range(4):
+        for h in range(4):
+            halving(h, j).wait_send()
+        for tile in early + middle:
+            doubling(tile, j).wait_send()
     pltpu.make_async_copy(whole_tiles, whole_tiles, ag_send).wait()
 
 
@@ -598,27 +722,34 @@
             pltpu.VMEM((ROWS, W), F32),
             pltpu.VMEM((KP, W), BF16),
             pltpu.VMEM((KP, W), BF16),
-            pltpu.VMEM((7, 16, 16, W), F32),
-            pltpu.VMEM((7, 16, 16, W), F32),
+            pltpu.VMEM((3, 16, 16, W), F32),
+            pltpu.VMEM((3, 16, 16, W), F32),
+            pltpu.VMEM((4, 2, 2, 2, 2, 16, W), F32),
+            pltpu.VMEM((4, 2, 2, 2, 2, 16, W), F32),
             pltpu.VMEM((7, 16, W), F32),
             pltpu.VMEM((7, 16, W), F32),
             pltpu.VMEM((8, 16, W), F32),
             pltpu.VMEM((8, 16, W), F32),
             pltpu.VMEM((8, 16, W), F32),
-            pltpu.VMEM((8, 16, 16, W), F32),
+            pltpu.VMEM((6, 2, 2, 2, 2, 16, W), F32),
+            pltpu.VMEM((2, 16, 16, W), F32),
             pltpu.VMEM((32, 1, W), F32),
             pltpu.VMEM((1, 1, W), F32),
             pltpu.VMEM((8, 1, W), F32),
             dma((2, 2, 2)),
             dma((2, 2, 2)),
-            dma((6,)),
-            dma((6,)),
+            dma((8,)),
+            dma((8,)),
             dma((7,)),
             dma((7,)),
-            dma((3,)),
-            dma((3,)),
-            dma((11,)),
-            dma((11,)),
+            dma((2,)),
+            dma((2,)),
+            dma((4, 4)),
+            dma((4, 4)),
+            dma((6, 4)),
+            dma((6, 4)),
+            dma((16,)),
+            dma((16,)),
             dma,
             dma,
             dma,

time: 162 us -> 138 us (0.85)
  Pallas kernels: 156 us -> 133 us
    pallas_call x1, Pallas kernels: 156 us -> 133 us  [body(): pl.pallas_call(kernel, out_shape=jax.ShapeDtypeStruct((OWN, W), F32), in_...]
where the time goes in v1:
time: 138 us
  Pallas kernels  133 us (96%)
  local copies, waits for them, and re-layouts  5.14 us (4%)
    pallas_call x1, Pallas kernels, body(): pl.pallas_call(kernel, out_shape=jax.ShapeDtypeStruct((OWN, W), F32), in_...  133 us
    unnamed x2, local copies, waits for them, and re-layouts  5.14 us

profile of v1, /device:TPU:1, one launch (start us, length us, event | category | flops | bytes accessed | tf_op | source)
XLA Modules:
  0.0 138.2 jit_solution(5785872927952695946)
XLA Ops:
  0.0 3.2 %copy.7 = f32[1,729,729]{2,1,0:T(8,128)} copy(f32[1,729,729]{2,0,1:T(1,128)} %param.5) | data formatting | bytes 4251528
  3.2 133.0 %shard_map.46 = f32[648,256]{1,0:T(8,128)} custom-call(f32[648,256]{1,0:T(8,128)} %x_ref.1, f32[729,729]{1,0:T(8,128)} %bitcast.4, s32[1,729]{1,0:T(1,128)} %conn_ref.1, s32[1,81]{1,0:T(1,128)} %bitcast.5), custom_call_target="tpu_custom_call" | custom-call | tf_op jit(solution)/shard_map/pallas_call | solution.py:691
  136.2 2.0 %copy.9 = f32[648,256]{1,0:T(8,128)} copy(f32[648,256]{1,0:T(8,128)} %shard_map.46) | data formatting | bytes 1327104

commit v2 on v1

v2 whole, which is shorter than its diff:
```python
import functools

import jax
import jax.numpy as jnp
from jax import lax
from jax.experimental import pallas as pl
from jax.experimental.pallas import tpu as pltpu
from jax.sharding import PartitionSpec as P

DEGREE = 8
lowest = -1.0
cutoff = 1.5
ceiling = 4.5
eps_norm = 1e-06

F32 = jnp.float32
BF16 = jnp.bfloat16
MESH = pl.DeviceIdType.MESH

OWN = 648
CELL = 729
FACE = 81
TOTAL_ROWS = 20736
W = 256
HALF = 128
KP = 768
LOW = 567
REG_L = 560
REG_G = 648
REG = 88
REG_END = 736
INT = 560
CUT = 512
ROWS = 656
SOON = 488
PART = 320


def coefficients():
    half_width = (ceiling - cutoff) / 2.0
    centre = (ceiling + cutoff) / 2.0
    sigma_one = half_width / (lowest - centre)
    table = [(sigma_one / half_width, 0.0)]
    now = sigma_one
    for _ in range(DEGREE - 1):
        nxt = 1.0 / (2.0 / sigma_one - now)
        table.append((2.0 * nxt / half_width, now * nxt))
        now = nxt
    return centre, table


CENTRE, TABLE = coefficients()


def chosen(t, which):
    if isinstance(t, int):
        return TABLE[t][which]
    value = jnp.float32(TABLE[0][which])
    for step in range(1, DEGREE):
        value = jnp.where(t == step, jnp.float32(TABLE[step][which]), value)
    return value


def split2(value):
    high = value.astype(BF16)
    low = (value - high.astype(F32)).astype(BF16)
    return high, low


def dot(left, right):
    return jnp.dot(left, right, preferred_element_type=F32)


def dot_nt(left, right):
    return lax.dot_general(left, right, (((1,), (1,)), ((), ())), preferred_element_type=F32)


def iota(shape, dim):
    return lax.broadcasted_iota(jnp.int32, shape, dim)


def one_hot(position, shape, dim):
    return jnp.where(iota(shape, dim).astype(F32) == position, 1.0, 0.0).astype(BF16)


def kernel(
    x_ref, a_ref, conn_ref, faces_ref, out_ref,
    amat, a_sem, x_sem, irow, q, ah, al, bh, bl, mh, ml, qt, vcat, vbuf, xs, pre, pf,
    send_l, send_g, from_above, from_below,
    fall, ta_h, ta_l, tb_h, tb_l, stage_h, stage_l, acc, rot_h, rot_l,
    left_h, left_l, own_out,
    flat, flat_in, cube, cube_in0, cube_in1, mine, ex0, ex1, ex2, final, gathered, norms, nown, scales,
    halo_send, halo_recv, z_send, z_recv, d_send, d_recv,
    rs_send, rs_recv, c_send, c_recv, g_send, g_recv, ex_send, ex_recv, n_send, n_recv, s_send, s_recv,
):
    node = lax.axis_index("nodes")
    orb = lax.axis_index("orb")
    a = orb // 2
    c = orb % 2
    zl = (node // 4) % 2
    x, y = node % 4, node // 8
    bits = ((x // 2 + x % 2) % 2, x // 2, (y // 2 + y % 2) % 2, y // 2)
    flip = node + 4 - 8 * zl
    up = (node + 1) % 32
    down = (node + 31) % 32
    has_above = jnp.where(node < 31, jnp.float32(1.0), jnp.float32(0.0))
    has_below = jnp.where(node > 0, jnp.float32(1.0), jnp.float32(0.0))

    def orb_at(da, dc):
        other = c if dc == 0 else 1 - c
        return ((a + da) % 4) * 2 + other

    def number(corner):
        return corner[3] * 8 + corner[2] * 4 + corner[1] * 2 + corner[0]

    def node_of(corner):
        there_x = corner[1] * 2 + (corner[0] + corner[1]) % 2
        there_y = corner[3] * 2 + (corner[2] + corner[3]) % 2
        return there_y * 8 + zl * 4 + there_x

    sid = number(bits)

    matrix_copy = pltpu.make_async_copy(a_ref, amat, a_sem)
    orbitals_copy = pltpu.make_async_copy(x_ref, xs.at[0:OWN], x_sem)
    orbitals_copy.start()
    matrix_copy.start()
    from_above[...] = jnp.zeros(from_above.shape, F32)
    from_below[...] = jnp.zeros(from_below.shape, F32)

    barrier = pltpu.get_barrier_semaphore()

    def greet(k, _):
        pl.semaphore_signal(barrier, inc=1, device_id=((node + k) % 32, orb), device_id_type=MESH)
        return 0

    lax.fori_loop(1, 32, greet, 0)
    for k in range(1, 8):
        pl.semaphore_signal(barrier, inc=1, device_id=(node, orb_at(k // 2, k % 2)), device_id_type=MESH)
    for k in range(2, 8):
        pl.semaphore_signal(barrier, inc=1, device_id=(flip, orb_at(k // 2, k % 2)), device_id_type=MESH)

    irow[...] = jnp.full(irow.shape, 100000, jnp.int32)
    irow[0:1, 0:FACE] = faces_ref[...]
    face_row = irow[0:1, 0:128].astype(F32)
    irow[8:9, 0:CELL] = conn_ref[...]
    entry = irow[8:9, :].astype(F32)
    square = (128, 128)
    face_col = jnp.sum(
        jnp.where(iota(square, 0) == iota(square, 1), jnp.broadcast_to(face_row, square), 0.0), axis=1, keepdims=True
    )

    def position_row(number):
        shape = (128, KP)
        same = number == face_col
        hit = jnp.sum(jnp.where(same, iota(shape, 0).astype(F32) + 1.0, 0.0), axis=0, keepdims=True)
        below = jnp.sum(jnp.where(face_col < number, 1.0, 0.0), axis=0, keepdims=True)
        return jnp.where(hit > 0.0, LOW - 1.0 + hit, number - below)

    local = iota((1, KP), 1).astype(F32)
    local_pos = jnp.where(local < OWN, position_row(local), -1.0)
    cell_pos = jnp.where(entry < OWN, position_row(entry), jnp.where(entry < CELL, entry + 7.0, -1.0))

    q[...] = one_hot(local_pos, (KP, KP), 0)
    xs[OWN:KP, :] = jnp.zeros((KP - OWN, W), F32)
    orbitals_copy.wait()
    start = xs[...]
    x1 = start.astype(BF16)
    rest = start - x1.astype(F32)
    x2 = rest.astype(BF16)
    x3 = (rest - x2.astype(F32)).astype(BF16)
    vbuf[0, ...] = (dot(q[...], x1) + dot(q[...], x2)) + dot(q[...], x3)
    vbuf[1, ...] = jnp.zeros((KP, W), F32)

    q[...] = one_hot(cell_pos, (KP, KP), 0)
    matrix_copy.wait()
    high, low = split2(amat[...])
    ah[...] = jnp.zeros(ah.shape, BF16)
    al[...] = jnp.zeros(al.shape, BF16)
    ah[0:CELL, 0:CELL] = high
    al[0:CELL, 0:CELL] = low
    bh[...] = dot(q[...], ah[...]).astype(BF16)
    bl[...] = dot(q[...], al[...]).astype(BF16)

    pl.semaphore_wait(barrier, 31 + 7 + 6)

    def columns(chunk):
        return slice(chunk * HALF, (chunk + 1) * HALF)

    def halo(t, chunk, way):
        slot = (t + 2) % 2
        if way == 0:
            src, dst, target = send_l, from_above, down
        else:
            src, dst, target = send_g, from_below, up
        return pltpu.make_async_remote_copy(
            src_ref=src.at[slot, chunk],
            dst_ref=dst.at[slot, chunk],
            send_sem=halo_send.at[slot, chunk, way],
            recv_sem=halo_recv.at[slot, chunk, way],
            device_id=(target, orb),
            device_id_type=MESH,
        )

    def there(way):
        return node > 0 if way == 0 else node < 31

    def halo_start(t, chunk, way):
        @pl.when(there(way))
        def _():
            halo(t, chunk, way).start()

    def halo_in(t, chunk, way):
        @pl.when(there(1 - way))
        def _():
            halo(t, chunk, way).wait_recv()

    def halo_out(t, chunk, way):
        @pl.when(there(way))
        def _():
            halo(t, chunk, way).wait_send()

    for chunk in range(2):
        send_l[1, chunk] = vbuf[0, REG_L:REG_G, columns(chunk)]
        halo_start(-1, chunk, 0)

    mh[...] = dot_nt(bh[...], q[...]).astype(BF16)
    ml[...] = dot_nt(bl[...], q[...]).astype(BF16)

    reg_row = iota((REG, HALF), 0)
    mask = jnp.where(reg_row >= 7, 1.0, 0.0).astype(F32) * has_above

    def put(chunk, low_row, high_row, value):
        high, low = split2(value)
        vcat[chunk, low_row:high_row, 0:HALF] = high
        vcat[chunk, low_row:high_row, HALF:W] = low

    def product(chunk, rows, depth):
        both = dot(mh[rows, depth], vcat[chunk, depth, :])
        third = dot(ml[rows, depth], vcat[chunk, depth, 0:HALF])
        return (both[:, 0:HALF] + both[:, HALF:W]) + third

    def prepare(chunk):
        pre[chunk] = product(chunk, slice(INT, REG_END), slice(0, CUT))

    for chunk in range(2):
        put(chunk, 0, KP, vbuf[0, :, columns(chunk)])
        prepare(chunk)

    def faces_out(t, chunk):
        value = pre[chunk] + product(chunk, slice(INT, REG_END), slice(CUT, KP))
        pf[chunk] = value
        slot = (t + 2) % 2
        send_l[slot, chunk] = value[0:REG]
        send_g[slot, chunk] = value[REG : 2 * REG]
        halo_start(t, chunk, 0)
        halo_start(t, chunk, 1)

    def interior(t, chunk):
        now, old = t % 2, (t + 1) % 2
        total = product(chunk, slice(0, INT), slice(0, KP))
        cols = columns(chunk)
        fresh = (total - CENTRE * vbuf[now, 0:INT, cols]) * chosen(t, 0) - chosen(t, 1) * vbuf[old, 0:INT, cols]
        vbuf[old, 0:INT, cols] = fresh
        put(chunk, 0, INT, fresh)

    def faces_in(t, chunk):
        now, old = t % 2, (t + 1) % 2
        slot = t % 2
        halo_in(t, chunk, 0)
        halo_in(t, chunk, 1)
        cols = columns(chunk)
        lower = pf[chunk, 0:REG] + from_below[slot, chunk] * has_below
        upper = (pf[chunk, REG : 2 * REG] + from_above[slot, chunk]) * mask
        for rows, total in ((slice(REG_L, REG_G), lower), (slice(REG_G, REG_END), upper)):
            fresh = (total - CENTRE * vbuf[now, rows, cols]) * chosen(t, 0) - chosen(t, 1) * vbuf[old, rows, cols]
            vbuf[old, rows, cols] = fresh
            put(chunk, rows.start, rows.stop, fresh)

    def close(t):
        for chunk in range(2):
            halo_out(t, chunk, 0)
            halo_out(t, chunk, 1)

    for chunk in range(2):
        halo_in(-1, chunk, 0)
        ghost = from_above[1, chunk] * mask
        vbuf[0, REG_G:REG_END, columns(chunk)] = ghost
        put(chunk, REG_G, REG_END, ghost)
        faces_out(0, chunk)
    for chunk in range(2):
        interior(0, chunk)
        prepare(chunk)
    for chunk in range(2):
        halo_out(-1, chunk, 0)
    close(0)

    def step(t, _):
        for chunk in range(2):
            faces_in(t - 1, chunk)
            faces_out(t, chunk)
        for chunk in range(2):
            interior(t, chunk)
            prepare(chunk)
        close(t)
        return 0

    lax.fori_loop(1, DEGREE, step, 0)

    first, second = slice(0, PART), slice(PART, OWN)
    first_a, first_b = slice(0, 160), slice(160, PART)
    second_a, second_b = slice(PART, SOON), slice(SOON, OWN)
    hops = (
        (0, 6, first_a, 1),
        (0, 6, first_b, 1),
        (0, 2, second_a, 3),
        (0, 2, second_b, 3),
        (6, 4, first_a, 1),
        (6, 4, first_b, 1),
        (2, 4, second_a, 3),
        (2, 4, second_b, 3),
        (0, 6, slice(320, 440), 1),
        (0, 6, slice(440, 560), 1),
        (0, 6, slice(560, OWN), 1),
        (0, 2, slice(0, 120), 3),
        (0, 2, slice(120, 240), 3),
        (0, 2, slice(240, 320), 3),
    )
    crossings = (
        (0, slice(0, SOON)),
        (0, slice(SOON, OWN)),
        (6, first),
        (2, second),
        (4, first),
        (4, second),
        (6, second),
        (2, first),
    )

    def z_copy(index):
        src, dst, rows, da = hops[index]
        return pltpu.make_async_remote_copy(
            src_ref=fall.at[src, rows],
            dst_ref=fall.at[dst, rows],
            send_sem=z_send.at[index],
            recv_sem=z_recv.at[index],
            device_id=(node, orb_at(da, 0)),
            device_id_type=MESH,
        )

    def d_copy(index):
        slot, rows = crossings[index]
        return pltpu.make_async_remote_copy(
            src_ref=fall.at[slot, rows],
            dst_ref=fall.at[slot + 1, rows],
            send_sem=d_send.at[index],
            recv_sem=d_recv.at[index],
            device_id=(node, orb_at(0, 1)),
            device_id_type=MESH,
        )

    def z_in(*indices):
        for index in indices:
            z_copy(index).wait_recv()

    fall[0, 0:SOON, :] = vbuf[DEGREE % 2, 0:SOON, :]
    d_copy(0).start()
    d_copy(0).wait_recv()
    for index in (0, 2, 1):
        z_copy(index).start()
    for chunk in range(2):
        faces_in(DEGREE - 1, chunk)
    fall[0, SOON:OWN, :] = vbuf[DEGREE % 2, SOON:OWN, :]
    z_copy(3).start()
    d_copy(1).start()
    own = fall[0, 0:OWN, :]
    nown[0] = jnp.sum(own * own, axis=0, keepdims=True)
    norms[node] = nown[0]

    def norm_copy(k):
        return pltpu.make_async_remote_copy(
            src_ref=nown.at[0],
            dst_ref=norms.at[node],
            send_sem=n_send,
            recv_sem=n_recv,
            device_id=((node + k) % 32, orb),
            device_id_type=MESH,
        )

    def norm_start(k, _):
        norm_copy(k).start()
        return 0

    lax.fori_loop(1, 32, norm_start, 0)

    for k in range(8):
        fall[k, OWN:ROWS, :] = jnp.zeros((ROWS - OWN, W), F32)
    stage_h[...] = jnp.zeros(stage_h.shape, BF16)
    stage_l[...] = jnp.zeros(stage_l.shape, BF16)

    padded = (384, W)
    top = jnp.where(iota(padded, 0) < PART, fall[0, 0:384, :], 0.0)
    ta_h[...], ta_l[...] = split2(top.T)
    xs[...] = jnp.zeros(xs.shape, F32)
    xs[0 : OWN - PART, :] = fall[0, PART:OWN, :]
    tb_h[...], tb_l[...] = split2(xs[0:384, :].T)

    def half_gram(which, slot):
        rows = first if which == 0 else second
        high, low = split2(fall[slot, rows, :])
        count = rows.stop - rows.start
        stage_h[which, 0:count, :] = high
        stage_l[which, 0:count, :] = low
        left_h, left_l = (ta_h, ta_l) if which == 0 else (tb_h, tb_l)
        return (dot(left_h[...], stage_h[which]) + dot(left_h[...], stage_l[which])) + dot(left_l[...], stage_h[which])

    def keep(tile, value):
        if tile == 6:
            flat[...] = value.reshape(16, 16, W)
        else:
            cube[tile] = value.reshape(2, 2, 2, 2, 16, W)

    def rs_copy(k):
        to = [(bits[d] + k // 2**d) % 2 for d in range(4)]
        return pltpu.make_async_remote_copy(
            src_ref=flat.at[number(to)],
            dst_ref=flat_in.at[sid],
            send_sem=rs_send,
            recv_sem=rs_recv,
            device_id=(node_of(to), orb),
            device_id_type=MESH,
        )

    def rs_start():
        def one(k, _):
            rs_copy(k).start()
            return 0

        lax.fori_loop(1, 16, one, 0)

    def rs_sum():
        whole = flat_in.at[0:15]
        pltpu.make_async_copy(whole, whole, rs_recv).wait()
        flat_in[sid] = flat[sid]
        mine[6] = jnp.sum(flat_in[...], axis=0)

    def cube_index(values):
        return tuple(slice(None) if values[d] is None else values[d] for d in (3, 2, 1, 0))

    def rounds(tile):
        return ((0, 2), (1, 3)) if tile % 2 == 0 else ((1, 3), (0, 2))

    def peer(pair, way):
        to = list(bits)
        for d, flips in zip(pair, (way % 2, way // 2)):
            if flips:
                to[d] = 1 - bits[d]
        return to

    def halving(h, j, way):
        pairs = rounds(h)
        to = peer(pairs[j], way)
        src = [None] * 4
        for earlier in pairs[:j]:
            for d in earlier:
                src[d] = bits[d]
        for d in pairs[j]:
            src[d] = to[d]
        free = pairs[1 - j] if j == 0 else ()
        piece = tuple(src[d] if d not in free else None for d in range(4))
        return pltpu.make_async_remote_copy(
            src_ref=cube.at[(h,) + cube_index(piece)],
            dst_ref=(cube_in0 if j == 0 else cube_in1).at[(h, way - 1)],
            send_sem=c_send.at[h, j, way - 1],
            recv_sem=c_recv.at[h, j, way - 1],
            device_id=(node_of(to), orb),
            device_id_type=MESH,
        )

    def halving_start(h, j):
        for way in (3, 1, 2):
            halving(h, j, way).start()

    def halving_in(h, j):
        for way in (1, 2, 3):
            halving(h, j, way).wait_recv()
        pairs = rounds(h)
        kept = [None] * 4
        for done in pairs[: j + 1]:
            for d in done:
                kept[d] = bits[d]
        kept = (h,) + cube_index(kept)
        came = cube_in0 if j == 0 else cube_in1
        total = (cube[kept] + came[h, 0]) + (came[h, 1] + came[h, 2])
        if j == 0:
            cube[kept] = total
        else:
            mine[h] = total

    def doubling(tile, j, way):
        pairs = rounds(tile)
        which = [None] * 4
        for later in pairs[j:]:
            for d in later:
                which[d] = bits[d]
        where = (tile,) + cube_index(which)
        return pltpu.make_async_remote_copy(
            src_ref=gathered.at[where],
            dst_ref=gathered.at[where],
            send_sem=g_send.at[tile, j, way - 1],
            recv_sem=g_recv.at[tile, j, way - 1],
            device_id=(node_of(peer(pairs[j], way)), orb),
            device_id_type=MESH,
        )

    def doubling_start(tiles, j):
        for tile in tiles:
            if j == 0:
                gathered[(tile,) + cube_index(bits)] = final[tile]
            for way in (3, 1, 2):
                doubling(tile, j, way).start()

    def doubling_wait(tiles, j):
        for tile in tiles:
            for way in (1, 2, 3):
                doubling(tile, j, way).wait_recv()

    cross = jnp.where(a >= 2, 1 - c, c)
    partner = ((a + 2) % 4) * 2 + cross
    late = jnp.where(a >= 2, 1, 0)

    def ex_copies(group):
        lo, hi = ((0, 2), (2, 6), (6, 7))[group]
        copies = [
            pltpu.make_async_remote_copy(
                src_ref=mine.at[lo:hi],
                dst_ref=ex0.at[lo:hi],
                send_sem=ex_send.at[group],
                recv_sem=ex_recv.at[group],
                device_id=(flip, orb),
                device_id_type=MESH,
            )
        ]
        pairs = (
            (),
            ((2, 4, orb_at(3, 0)), (3, 5, orb_at(3, 1)), (4, 2, orb_at(1, 0)), (5, 3, orb_at(1, 1))),
            ((6, 7, partner),),
        )[group]
        for src, dst, who in pairs:
            for near in range(2):
                copies.append(
                    pltpu.make_async_remote_copy(
                        src_ref=mine.at[src],
                        dst_ref=(ex1, ex2)[near].at[dst],
                        send_sem=ex_send.at[2 * dst + near],
                        recv_sem=ex_recv.at[2 * dst + near],
                        device_id=(node if near == 0 else flip, who),
                        device_id_type=MESH,
                    )
                )
        return copies

    def ex_start(group):
        for copy in ex_copies(group):
            copy.start()

    def ex_in(group):
        for copy in ex_copies(group):
            copy.wait_recv()
        for tile in ((0, 1), (2, 3, 4, 5), (6, 7))[group]:
            if tile < 2 or tile == 6:
                final[tile] = mine[tile] + ex0[tile]
            elif tile == 7:
                final[tile] = ex1[tile] + ex2[tile]
            else:
                final[tile] = (mine[tile] + ex0[tile]) + (ex1[tile] + ex2[tile])

    keep(0, half_gram(0, 0) + half_gram(1, 0))
    halving_start(0, 0)
    d_copy(1).wait_recv()
    keep(1, half_gram(0, 1) + half_gram(1, 1))
    halving_start(1, 0)

    natural = iota((ROWS, 1), 0).astype(F32)
    face_lane = jnp.broadcast_to(face_row, (ROWS, 128))
    lane = iota((ROWS, 128), 1).astype(F32)
    hit = jnp.sum(jnp.where(face_lane == natural, lane + 1.0, 0.0), axis=1, keepdims=True)
    below = jnp.sum(jnp.where(face_lane < natural, 1.0, 0.0), axis=1, keepdims=True)
    back = jnp.where(hit > 0.0, LOW - 1.0 + hit, natural - below)
    qt[...] = one_hot(back, (ROWS, KP), 1)
    rot_h[ROWS:KP, :] = jnp.zeros((KP - ROWS, W), BF16)
    rot_l[ROWS:KP, :] = jnp.zeros((KP - ROWS, W), BF16)

    z_in(0)
    z_copy(4).start()
    z_in(2)
    z_copy(6).start()
    for tile in (0, 1):
        halving_in(tile, 0)
        halving_start(tile, 1)
    for tile in (0, 1):
        halving_in(tile, 1)
    ex_start(0)
    z_in(1)
    z_copy(5).start()
    d_copy(2).start()
    z_in(3)
    z_copy(7).start()
    d_copy(3).start()
    keep(2, half_gram(0, 6))
    halving_start(2, 0)
    keep(4, half_gram(1, 2).T)
    halving_start(4, 0)
    d_copy(2).wait_recv()
    keep(3, half_gram(0, 7))
    halving_start(3, 0)
    d_copy(3).wait_recv()
    keep(5, half_gram(1, 3).T)
    halving_start(5, 0)

    whole_norms = norms.at[0:31]
    pltpu.make_async_copy(whole_norms, whole_norms, n_recv).wait()
    scales[0] = lax.rsqrt(jnp.sum(norms[...], axis=0) / TOTAL_ROWS + eps_norm)

    def scale_copy(k):
        da, dc = k // 2, k % 2
        return pltpu.make_async_remote_copy(
            src_ref=scales.at[0],
            dst_ref=scales.at[((4 - da) % 4) * 2 + dc],
            send_sem=s_send.at[k],
            recv_sem=s_recv.at[k],
            device_id=(node, orb_at(da, dc)),
            device_id_type=MESH,
        )

    for k in range(1, 8):
        scale_copy(k).start()

    def laid_out(slot):
        scale = scales[slot]
        value = fall[slot] if slot == 0 else fall[slot] * (scale * scale)
        high, low = split2(value)
        rot_h[0:ROWS, :] = high
        rot_l[0:ROWS, :] = low
        return dot(qt[...], rot_h[...]), dot(qt[...], rot_l[...])

    def lay_out(slot):
        high, low = laid_out(slot)
        left_h[slot] = high.astype(BF16)
        left_l[slot] = low.astype(BF16)

    def rotated(slot, tile, transposed):
        right_h, right_l = split2(gathered[tile].reshape(W, W))
        times = dot_nt if transposed else dot
        return (times(left_h[slot], right_h) + times(left_h[slot], right_l)) + times(left_l[slot], right_h)

    early, middle, last = (0, 1), (2, 3, 4, 5), (6, 7)
    for tile in middle:
        halving_in(tile, 0)
        halving_start(tile, 1)
    z_copy(8).start()
    z_copy(11).start()
    scale_copy(1).wait_recv()
    high, low = laid_out(0)
    own_out[...] = (high + low) * (1.5 * scales[0])
    square_own = scales[0] * scales[0]
    high, low = split2((high + low) * square_own)
    left_h[0] = high
    left_l[0] = low
    lay_out(1)
    for tile in middle:
        halving_in(tile, 1)
    ex_start(1)
    z_copy(9).start()
    z_copy(12).start()
    ex_in(0)
    doubling_start(early, 0)
    z_in(4, 5)
    d_copy(4).start()
    z_in(6, 7)
    d_copy(5).start()
    d_copy(4).wait_recv()
    d_copy(5).wait_recv()
    keep(6, half_gram(0, 4 + late) + half_gram(1, 4 + late))
    rs_start()
    doubling_wait(early, 0)
    doubling_start(early, 1)
    ex_in(1)
    doubling_start(middle, 0)
    for k in range(2, 8):
        scale_copy(k).wait_recv()
    lay_out(4)
    lay_out(5)
    rs_sum()
    ex_start(2)
    z_copy(10).start()
    z_copy(13).start()
    doubling_wait(middle, 0)
    doubling_start(middle, 1)
    doubling_wait(early, 1)
    acc[...] = rotated(0, 0, False)
    acc[...] += rotated(1, 1, True)
    ex_in(2)
    doubling_start(last, 0)
    z_in(8, 9, 10)
    d_copy(6).start()
    z_in(11, 12, 13)
    d_copy(7).start()
    lay_out(2)
    lay_out(6)
    doubling_wait(last, 0)
    doubling_start(last, 1)
    d_copy(6).wait_recv()
    lay_out(7)
    d_copy(7).wait_recv()
    lay_out(3)
    doubling_wait(middle, 1)
    acc[...] += rotated(2, 4, False)
    acc[...] += rotated(6, 2, True)
    acc[...] += rotated(7, 3, True)
    acc[...] += rotated(3, 5, False)
    doubling_wait(last, 1)
    acc[...] += rotated(4 + late, 6, True)
    acc[...] += rotated(5 - late, 7, False)
    result = own_out[...] - acc[...] * ((0.5 / TOTAL_ROWS) * scales[0])
    out_ref[...] = result[0:OWN, :]

    for index in range(14):
        z_copy(index).wait_send()
    for index in range(8):
        d_copy(index).wait_send()
    for k in range(1, 8):
        scale_copy(k).wait_send()
    pltpu.make_async_copy(whole_norms, whole_norms, n_send).wait()
    sent = flat_in.at[0:15]
    pltpu.make_async_copy(sent, sent, rs_send).wait()
    for group in range(3):
        for copy in ex_copies(group):
            copy.wait_send()
    for j in range(2):
        for way in (1, 2, 3):
            for tile in range(6):
                halving(tile, j, way).wait_send()
            for tile in range(8):
                doubling(tile, j, way).wait_send()


def body(orbitals, cell_matrix, connectivity, face_nodes):
    vmem = pl.BlockSpec(memory_space=pltpu.VMEM)
    anywhere = pl.BlockSpec(memory_space=pl.ANY)
    dma = pltpu.SemaphoreType.DMA
    return pl.pallas_call(
        kernel,
        out_shape=jax.ShapeDtypeStruct((OWN, W), F32),
        in_specs=[anywhere, anywhere, vmem, vmem],
        out_specs=vmem,
        scratch_shapes=[
            pltpu.VMEM((CELL, CELL), F32),
            dma,
            dma,
            pltpu.VMEM((16, KP), jnp.int32),
            pltpu.VMEM((KP, KP), BF16),
            pltpu.VMEM((KP, KP), BF16),
            pltpu.VMEM((KP, KP), BF16),
            pltpu.VMEM((KP, KP), BF16),
            pltpu.VMEM((KP, KP), BF16),
            pltpu.VMEM((KP, KP), BF16),
            pltpu.VMEM((KP, KP), BF16),
            pltpu.VMEM((ROWS, KP), BF16),
            pltpu.VMEM((2, KP, W), BF16),
            pltpu.VMEM((2, KP, W), F32),
            pltpu.VMEM((KP, W), F32),
            pltpu.VMEM((2, 2 * REG, HALF), F32),
            pltpu.VMEM((2, 2 * REG, HALF), F32),
            pltpu.VMEM((2, 2, REG, HALF), F32),
            pltpu.VMEM((2, 2, REG, HALF), F32),
            pltpu.VMEM((2, 2, REG, HALF), F32),
            pltpu.VMEM((2, 2, REG, HALF), F32),
            pltpu.VMEM((8, ROWS, W), F32),
            pltpu.VMEM((W, 384), BF16),
            pltpu.VMEM((W, 384), BF16),
            pltpu.VMEM((W, 384), BF16),
            pltpu.VMEM((W, 384), BF16),
            pltpu.VMEM((2, 384, W), BF16),
            pltpu.VMEM((2, 384, W), BF16),
            pltpu.VMEM((ROWS, W), F32),
            pltpu.VMEM((KP, W), BF16),
            pltpu.VMEM((KP, W), BF16),
            pltpu.VMEM((8, ROWS, W), BF16),
            pltpu.VMEM((8, ROWS, W), BF16),
            pltpu.VMEM((ROWS, W), F32),
            pltpu.VMEM((16, 16, W), F32),
            pltpu.VMEM((16, 16, W), F32),
            pltpu.VMEM((6, 2, 2, 2, 2, 16, W), F32),
            pltpu.VMEM((6, 3, 2, 2, 16, W), F32),
            pltpu.VMEM((6, 3, 16, W), F32),
            pltpu.VMEM((7, 16, W), F32),
            pltpu.VMEM((7, 16, W), F32),
            pltpu.VMEM((8, 16, W), F32),
            pltpu.VMEM((8, 16, W), F32),
            pltpu.VMEM((8, 16, W), F32),
            pltpu.VMEM((8, 2, 2, 2, 2, 16, W), F32),
            pltpu.VMEM((32, 1, W), F32),
            pltpu.VMEM((1, 1, W), F32),
            pltpu.VMEM((8, 1, W), F32),
            dma((2, 2, 2)),
            dma((2, 2, 2)),
            dma((14,)),
            dma((14,)),
            dma((8,)),
            dma((8,)),
            dma,
            dma,
            dma((6, 2, 3)),
            dma((6, 2, 3)),
            dma((8, 2, 3)),
            dma((8, 2, 3)),
            dma((16,)),
            dma((16,)),
            dma,
            dma,
            dma((8,)),
            dma((8,)),
        ],
        compiler_params=pltpu.CompilerParams(
            collective_id=0, has_side_effects=True, vmem_limit_bytes=60 * 1024 * 1024
        ),
    )(orbitals, cell_matrix[0], connectivity, face_nodes.reshape(1, FACE))


def solution(mesh):
    return jax.shard_map(
        body,
        mesh=mesh,
        in_specs=(P("nodes", "orb"), P("nodes", None, None), P("nodes", None), P("nodes")),
        out_specs=P("nodes", "orb"),
        check_vma=False,
    )
```

time: 138 us -> 130 us (0.942)
  Pallas kernels: 133 us -> 125 us
    pallas_call x1, Pallas kernels: 133 us -> 125 us  [body(): pl.pallas_call(kernel, out_shape=jax.ShapeDtypeStruct((OWN, W), F32), in_...]
where the time goes in v2:
time: 130 us
  Pallas kernels  125 us (96%)
  local copies, waits for them, and re-layouts  5.14 us (4%)
    pallas_call x1, Pallas kernels, body(): pl.pallas_call(kernel, out_shape=jax.ShapeDtypeStruct((OWN, W), F32), in_...  125 us
    unnamed x2, local copies, waits for them, and re-layouts  5.14 us

profile of v2, /device:TPU:1, one launch (start us, length us, event | category | flops | bytes accessed | tf_op | source)
XLA Modules:
  0.0 130.2 jit_solution(6069606697449278248)
XLA Ops:
  0.0 3.2 %copy.7 = f32[1,729,729]{2,1,0:T(8,128)} copy(f32[1,729,729]{2,0,1:T(1,128)} %param.5) | data formatting | bytes 4251528
  3.2 125.0 %shard_map.46 = f32[648,256]{1,0:T(8,128)} custom-call(f32[648,256]{1,0:T(8,128)} %x_ref.1, f32[729,729]{1,0:T(8,128)} %bitcast.4, s32[1,729]{1,0:T(1,128)} %conn_ref.1, s32[1,81]{1,0:T(1,128)} %bitcast.5), custom_call_target="tpu_custom_call" | custom-call | tf_op jit(solution)/shard_map/pallas_call | solution.py:751
  128.2 2.0 %copy.9 = f32[648,256]{1,0:T(8,128)} copy(f32[648,256]{1,0:T(8,128)} %shard_map.46) | data formatting | bytes 1327104

commit v3 on v2

--- a/solution.py
+++ b/solution.py
@@ -606,6 +606,8 @@
     z_in(3)
     z_copy(7).start()
     d_copy(3).start()
+    z_copy(8).start()
+    z_copy(11).start()
     keep(2, half_gram(0, 6))
     halving_start(2, 0)
     keep(4, half_gram(1, 2).T)
@@ -657,8 +659,21 @@
     for tile in middle:
         halving_in(tile, 0)
         halving_start(tile, 1)
-    z_copy(8).start()
-    z_copy(11).start()
+    z_in(4, 5)
+    d_copy(4).start()
+    z_in(6, 7)
+    d_copy(5).start()
+    for tile in middle:
+        halving_in(tile, 1)
+    ex_start(1)
+    z_copy(9).start()
+    z_copy(12).start()
+    d_copy(4).wait_recv()
+    d_copy(5).wait_recv()
+    keep(6, half_gram(0, 4 + late) + half_gram(1, 4 + late))
+    rs_start()
+    ex_in(0)
+    doubling_start(early, 0)
     scale_copy(1).wait_recv()
     high, low = laid_out(0)
     own_out[...] = (high + low) * (1.5 * scales[0])
@@ -667,33 +682,18 @@
     left_h[0] = high
     left_l[0] = low
     lay_out(1)
-    for tile in middle:
-        halving_in(tile, 1)
-    ex_start(1)
-    z_copy(9).start()
-    z_copy(12).start()
-    ex_in(0)
-    doubling_start(early, 0)
-    z_in(4, 5)
-    d_copy(4).start()
-    z_in(6, 7)
-    d_copy(5).start()
-    d_copy(4).wait_recv()
-    d_copy(5).wait_recv()
-    keep(6, half_gram(0, 4 + late) + half_gram(1, 4 + late))
-    rs_start()
     doubling_wait(early, 0)
     doubling_start(early, 1)
     ex_in(1)
     doubling_start(middle, 0)
+    rs_sum()
+    ex_start(2)
+    z_copy(10).start()
+    z_copy(13).start()
     for k in range(2, 8):
         scale_copy(k).wait_recv()
     lay_out(4)
     lay_out(5)
-    rs_sum()
-    ex_start(2)
-    z_copy(10).start()
-    z_copy(13).start()
     doubling_wait(middle, 0)
     doubling_start(middle, 1)
     doubling_wait(early, 1)

time: 130 us -> 129 us (level)
    pallas_call x1, Pallas kernels: 125 us -> 124 us  [body(): pl.pallas_call(kernel, out_shape=jax.ShapeDtypeStruct((OWN, W), F32), in_...]
where the time goes in v3:
time: 129 us
  Pallas kernels  124 us (96%)
  local copies, waits for them, and re-layouts  5.14 us (4%)
    pallas_call x1, Pallas kernels, body(): pl.pallas_call(kernel, out_shape=jax.ShapeDtypeStruct((OWN, W), F32), in_...  124 us
    unnamed x2, local copies, waits for them, and re-layouts  5.14 us

profile of v3, /device:TPU:1, one launch (start us, length us, event | category | flops | bytes accessed | tf_op | source)
XLA Modules:
  0.0 128.7 jit_solution(7834041383649581689)
XLA Ops:
  0.0 3.2 %copy.7 = f32[1,729,729]{2,1,0:T(8,128)} copy(f32[1,729,729]{2,0,1:T(1,128)} %param.5) | data formatting | bytes 4251528
  3.2 123.5 %shard_map.46 = f32[648,256]{1,0:T(8,128)} custom-call(f32[648,256]{1,0:T(8,128)} %x_ref.1, f32[729,729]{1,0:T(8,128)} %bitcast.4, s32[1,729]{1,0:T(1,128)} %conn_ref.1, s32[1,81]{1,0:T(1,128)} %bitcast.5), custom_call_target="tpu_custom_call" | custom-call | tf_op jit(solution)/shard_map/pallas_call | solution.py:751
  126.7 2.0 %copy.9 = f32[648,256]{1,0:T(8,128)} copy(f32[648,256]{1,0:T(8,128)} %shard_map.46) | data formatting | bytes 1327104
